TPU v7x, 32 devices: a whole 2x2x4 slice. The times are simulated.
32 devices in a mesh: dp: 8 (over z, y), tensor: 4 (over x, core).
Axes of the slice: x: 2, y: 2, z: 4, core: 2. Of those that a mesh axis runs over, the one named last changes fastest.
Arguments:
- tokens: bfloat16 [8192, 1024], P('dp'), may hold values from -6 to 6
- cotangent: bfloat16 [8192, 1024], P('dp'), may hold values from -6 to 6
- norm_params: float32 [4, 1024], replicated, may hold values from 0.25 to 1.75
- attention_weight: bfloat16 [1024, 3, 1024], P('dp', None, 'tensor'), may hold values from -0.1875 to 0.1875
- attention_bias: float32 [3, 1024], P(None, 'tensor'), may hold values from -3 to 3
- merge_weight: bfloat16 [1024, 1024], P('dp', 'tensor'), may hold values from -1.5 to 1.5
- branch_bias: float32 [2, 1024], replicated, may hold values from -3 to 3
- up_weight: bfloat16 [1024, 4096], P('dp', 'tensor'), may hold values from -0.1875 to 0.1875
- up_bias: float32 [4096], P('tensor'), may hold values from -3 to 3
- down_weight: bfloat16 [1024, 4096], P('dp', 'tensor'), may hold values from -0.09375 to 0.09375
- prefix_ids: int32 [10], replicated, may hold values from 0 to 9, each once
- prefix_table: float32 [10, 1024], replicated, may hold values from -1.25 to 1.25
- encoder_weight: float32 [1024, 512], P('dp'), may hold values from -0.625 to 0.625
- encoder_bias: float32 [512], replicated, may hold values from -0.625 to 0.625
- decoder_weight: float32 [512, 2, 1024], P('dp', None, 'tensor'), may hold values from -0.625 to 0.625
- decoder_bias: float32 [2, 1024], P(None, 'tensor'), may hold values from -0.625 to 0.625
- first_table: float32 [10, 1024], replicated, may hold values from -1.9073486e-06 to 1.9073486e-06
- second_table: float32 [10, 1024], replicated, may hold values from 5.3138434e-15 to 8.5369944e-14
- first_encoder: float32 [1024, 512], P('dp'), may hold values from -5.9604645e-07 to 5.9604645e-07
- second_encoder: float32 [1024, 512], P('dp'), may hold values from 3.8329363e-16 to 6.0978533e-15
- first_encoder_bias: float32 [512], replicated, may hold values from -3.33786e-06 to 3.33786e-06
- second_encoder_bias: float32 [512], replicated, may hold values from 1.0540575e-14 to 1.6899766e-13
- first_decoder: float32 [512, 2, 1024], P('dp', None, 'tensor'), may hold values from -4.7683716e-07 to 4.7683716e-07
- second_decoder: float32 [512, 2, 1024], P('dp', None, 'tensor'), may hold values from 2.230072e-16 to 3.5716e-15
- first_decoder_bias: float32 [2, 1024], P(None, 'tensor'), may hold values from -9.536743e-07 to 9.536743e-07
- second_decoder_bias: float32 [2, 1024], P(None, 'tensor'), may hold values from 8.885443e-16 to 1.42864e-14
Outputs:
- output: bfloat16 [8192, 1024], P(('dp', 'tensor'))
- input_grad: bfloat16 [8192, 1024], P(('dp', 'tensor'))
- grad_norm: float32 [], replicated
- new_table: float32 [10, 1024], replicated
- new_first_table: float32 [10, 1024], replicated
- new_second_table: float32 [10, 1024], replicated
- new_encoder: float32 [1024, 512], P('dp')
- new_first_encoder: float32 [1024, 512], P('dp')
- new_second_encoder: float32 [1024, 512], P('dp')
- new_encoder_bias: float32 [512], replicated
- new_first_encoder_bias: float32 [512], replicated
- new_second_encoder_bias: float32 [512], replicated
- new_decoder: float32 [512, 2, 1024], P('dp', None, 'tensor')
- new_first_decoder: float32 [512, 2, 1024], P('dp', None, 'tensor')
- new_second_decoder: float32 [512, 2, 1024], P('dp', None, 'tensor')
- new_decoder_bias: float32 [2, 1024], P(None, 'tensor')
- new_first_decoder_bias: float32 [2, 1024], P(None, 'tensor')
- new_second_decoder_bias: float32 [2, 1024], P(None, 'tensor')
Inputs may be any that keep to these rules, and one draw needn't show every extreme that they name: `prefix_ids`: every table row is used by exactly one prefix position.
All inputs are finite; a program needn't handle non-finite values.
Results may differ from a plain program's by a relative error of at most 0.017.
Values may be sent and summed in bfloat16 or wider, within the bound.
No kernel may reach another device: no remote copies, remote signals or barrier semaphores. Data moves between devices by JAX's collectives and lax.ppermute only.
A program may use at most 128 MiB of HBM per device.

v0:
```python
import jax
import jax.numpy as jnp
from jax import lax
from jax.sharding import PartitionSpec as P

HD = 64
PRE = 10
SEQ = 1024
STEP = 10
NORM_EPS = 1e-05
CLIP_LIMIT = 0.001
LEARN_RATE = 0.05
WEIGHT_DECAY = 0.01
BETA_FIRST = 0.9
BETA_SECOND = 0.999
ADAM_EPS = 1e-08
MASKED = -1e30
GELU_COEF = 0.7978845608028654


def layer_norm(rows, gain, shift):
    center = jnp.mean(rows, axis=-1, keepdims=True)
    offsets = rows - center
    spread = jnp.mean(offsets * offsets, axis=-1, keepdims=True)
    return offsets * lax.rsqrt(spread + NORM_EPS) * gain + shift


def norm_back(rows, gain, shift, grad_rows):
    _, pull_back = jax.vjp(lambda values: layer_norm(values, gain, shift), rows)
    return pull_back(grad_rows)[0]


def gelu_tanh(values):
    return (
        0.5 * values * (1.0 + jnp.tanh(GELU_COEF * (values + 0.044715 * values * values * values)))
    )


def adam_update(weight, grad, first, second, factor):
    clipped = grad * factor
    new_first = BETA_FIRST * first + (1.0 - BETA_FIRST) * clipped
    new_second = BETA_SECOND * second + (1.0 - BETA_SECOND) * clipped * clipped
    fix_first = 1.0 - BETA_FIRST**STEP
    fix_second = 1.0 - BETA_SECOND**STEP
    new_weight = weight * (1.0 - LEARN_RATE * WEIGHT_DECAY) - LEARN_RATE * (
        new_first / fix_first
    ) / (jnp.sqrt(new_second / fix_second) + ADAM_EPS)
    return (new_weight, new_first, new_second)


def score_blocks(query_rows, keys, prefix_keys, offset, finish, score_scale):
    pre_scores = (
        jnp.einsum("qhe,jhe->hqj", query_rows, prefix_keys, preferred_element_type=jnp.float32)
        * score_scale
    )
    own_scores = (
        jnp.einsum("qhe,khe->hqk", query_rows, keys[:finish], preferred_element_type=jnp.float32)
        * score_scale
    )
    visible = (offset + jnp.arange(finish - offset))[:, None] >= jnp.arange(finish)[None, :]
    own_scores = jnp.where(visible[None], own_scores, MASKED)
    return (pre_scores, own_scores)


def attend_forward(queries, keys, values, prefix_keys, prefix_values):
    length = queries.shape[0]
    block_rows = min(512, length)
    score_scale = float(queries.shape[2]) ** (-0.5)
    mixtures = []
    log_sums = []
    for offset in range(0, length, block_rows):
        finish = offset + block_rows
        pre_scores, own_scores = score_blocks(
            queries[offset:finish], keys, prefix_keys, offset, finish, score_scale
        )
        highest = jnp.maximum(jnp.max(pre_scores, -1), jnp.max(own_scores, -1))
        pre_exp = jnp.exp(pre_scores - highest[..., None])
        own_exp = jnp.exp(own_scores - highest[..., None])
        totals = jnp.sum(pre_exp, -1) + jnp.sum(own_exp, -1)
        pre_prob = (pre_exp / totals[..., None]).astype(jnp.bfloat16)
        own_prob = (own_exp / totals[..., None]).astype(jnp.bfloat16)
        mixture = jnp.einsum(
            "hqj,jhe->qhe", pre_prob, prefix_values, preferred_element_type=jnp.float32
        )
        mixture = mixture + jnp.einsum(
            "hqk,khe->qhe", own_prob, values[:finish], preferred_element_type=jnp.float32
        )
        mixtures.append(mixture)
        log_sums.append(highest + jnp.log(totals))
    return (jnp.concatenate(mixtures, 0), jnp.concatenate(log_sums, 1))


def attend_backward(queries, keys, values, prefix_keys, prefix_values, grad_out, log_sums):
    length = queries.shape[0]
    block_rows = min(512, length)
    score_scale = float(queries.shape[2]) ** (-0.5)
    grad_queries = []
    grad_keys = jnp.zeros(keys.shape, jnp.float32)
    grad_values = jnp.zeros(values.shape, jnp.float32)
    grad_pre_keys = jnp.zeros(prefix_keys.shape, jnp.float32)
    grad_pre_values = jnp.zeros(prefix_values.shape, jnp.float32)
    for offset in range(0, length, block_rows):
        finish = offset + block_rows
        query_rows = queries[offset:finish]
        grad_rows = grad_out[offset:finish]
        pre_scores, own_scores = score_blocks(
            query_rows, keys, prefix_keys, offset, finish, score_scale
        )
        block_sums = log_sums[:, offset:finish, None]
        pre_prob = jnp.exp(pre_scores - block_sums)
        own_prob = jnp.exp(own_scores - block_sums)
        pre_dprob = jnp.einsum(
            "qhe,jhe->hqj", grad_rows, prefix_values, preferred_element_type=jnp.float32
        )
        own_dprob = jnp.einsum(
            "qhe,khe->hqk", grad_rows, values[:finish], preferred_element_type=jnp.float32
        )
        inner = jnp.sum(pre_prob * pre_dprob, -1) + jnp.sum(own_prob * own_dprob, -1)
        pre_dscore = (pre_prob * (pre_dprob - inner[..., None])).astype(jnp.bfloat16)
        own_dscore = (own_prob * (own_dprob - inner[..., None])).astype(jnp.bfloat16)
        grad_query = jnp.einsum(
            "hqj,jhe->qhe", pre_dscore, prefix_keys, preferred_element_type=jnp.float32
        )
        grad_query = grad_query + jnp.einsum(
            "hqk,khe->qhe", own_dscore, keys[:finish], preferred_element_type=jnp.float32
        )
        grad_queries.append(grad_query * score_scale)
        grad_keys = grad_keys.at[:finish].add(
            jnp.einsum("hqk,qhe->khe", own_dscore, query_rows, preferred_element_type=jnp.float32)
            * score_scale
        )
        grad_values = grad_values.at[:finish].add(
            jnp.einsum(
                "hqk,qhe->khe",
                own_prob.astype(jnp.bfloat16),
                grad_rows,
                preferred_element_type=jnp.float32,
            )
        )
        grad_pre_keys = (
            grad_pre_keys
            + jnp.einsum("hqj,qhe->jhe", pre_dscore, query_rows, preferred_element_type=jnp.float32)
            * score_scale
        )
        grad_pre_values = grad_pre_values + jnp.einsum(
            "hqj,qhe->jhe",
            pre_prob.astype(jnp.bfloat16),
            grad_rows,
            preferred_element_type=jnp.float32,
        )
    grad_seq = jnp.stack([jnp.concatenate(grad_queries, 0), grad_keys, grad_values], 1)
    grad_prefix = jnp.stack([grad_pre_keys, grad_pre_values], 1)
    return (grad_seq, grad_prefix)


def on_device(
    tokens,
    cotangent,
    norm_params,
    attention_weight,
    attention_bias,
    merge_weight,
    branch_bias,
    up_weight,
    up_bias,
    down_weight,
    prefix_ids,
    prefix_table,
    encoder_weight,
    encoder_bias,
    decoder_weight,
    decoder_bias,
    first_table,
    second_table,
    first_encoder,
    second_encoder,
    first_encoder_bias,
    second_encoder_bias,
    first_decoder,
    second_decoder,
    first_decoder_bias,
    second_decoder_bias,
):
    highest_prec = lax.Precision.HIGHEST
    dp_index = lax.axis_index("dp")
    tok_rows = tokens.shape[0]
    local_width = merge_weight.shape[1]
    local_heads = local_width // HD
    sequences = tok_rows // SEQ
    share = tok_rows // lax.axis_size("tensor")
    row_start = lax.axis_index("tensor") * share
    gathered = (
        lax.all_gather(attention_weight, "dp", axis=0, tiled=True),
        lax.all_gather(merge_weight, "dp", axis=0, tiled=True),
        lax.all_gather(up_weight, "dp", axis=0, tiled=True),
        lax.all_gather(down_weight, "dp", axis=0, tiled=True),
        lax.all_gather(encoder_weight.astype(jnp.bfloat16), "dp", axis=0, tiled=True),
        lax.all_gather(decoder_weight.astype(jnp.bfloat16), "dp", axis=0, tiled=True),
    )
    attend_full, merge_full, up_full, down_full, encoder_full, decoder_full = gathered
    onehot = (prefix_ids[:, None] == jnp.arange(PRE, dtype=jnp.int32)[None, :]).astype(jnp.float32)
    selected = jnp.dot(onehot, prefix_table, precision=highest_prec)
    selected_low = selected.astype(jnp.bfloat16)
    encoded = jnp.dot(selected_low, encoder_full, preferred_element_type=jnp.float32) + encoder_bias
    hidden_prefix = jnp.tanh(encoded)
    hidden_low = hidden_prefix.astype(jnp.bfloat16)
    prefix_kv = (
        jnp.einsum("jp,pcm->jcm", hidden_low, decoder_full, preferred_element_type=jnp.float32)
        + decoder_bias[None]
    )
    prefix_kv = prefix_kv.astype(jnp.bfloat16).reshape(PRE, 2, local_heads, HD)
    prefix_keys = prefix_kv[:, 0]
    prefix_values = prefix_kv[:, 1]
    inputs = tokens.astype(jnp.float32)

    def forward_sequence(seq_rows):
        return attend_forward(
            seq_rows[:, 0], seq_rows[:, 1], seq_rows[:, 2], prefix_keys, prefix_values
        )

    def front(attend_mat, merge_mat, up_mat):
        normed_one = layer_norm(inputs, norm_params[0], norm_params[1]).astype(jnp.bfloat16)
        projected = (
            jnp.einsum("td,dcm->tcm", normed_one, attend_mat, preferred_element_type=jnp.float32)
            + attention_bias[None]
        )
        projected = projected.astype(jnp.bfloat16).reshape(sequences, SEQ, 3, local_heads, HD)
        mixtures, log_sums = lax.map(forward_sequence, projected)
        mixture = mixtures.reshape(tok_rows, local_width).astype(jnp.bfloat16)
        merged_part = jnp.einsum(
            "tm,dm->td", mixture, merge_mat, preferred_element_type=jnp.float32
        )
        merged = lax.psum(merged_part.astype(jnp.bfloat16), "tensor").astype(jnp.float32)
        resid = inputs + merged + branch_bias[0]
        normed_two = layer_norm(resid, norm_params[2], norm_params[3]).astype(jnp.bfloat16)
        hidden_pre = jnp.dot(normed_two, up_mat, preferred_element_type=jnp.float32) + up_bias
        return (projected, log_sums, resid, hidden_pre)

    projected, log_sums, resid, hidden_pre = front(attend_full, merge_full, up_full)
    hidden_act = gelu_tanh(hidden_pre).astype(jnp.bfloat16)
    branch_part = jnp.einsum("tf,df->td", hidden_act, down_full, preferred_element_type=jnp.float32)
    branch_out = lax.psum(branch_part.astype(jnp.bfloat16), "tensor").astype(jnp.float32)
    output_rows = (
        lax.dynamic_slice_in_dim(resid, row_start, share, 0)
        + lax.dynamic_slice_in_dim(branch_out, row_start, share, 0)
        + branch_bias[1]
    )
    regathered = (
        lax.all_gather(attention_weight, "dp", axis=0, tiled=True),
        lax.all_gather(merge_weight, "dp", axis=0, tiled=True),
        lax.all_gather(up_weight, "dp", axis=0, tiled=True),
        lax.all_gather(down_weight, "dp", axis=0, tiled=True),
        lax.all_gather(encoder_weight.astype(jnp.bfloat16), "dp", axis=0, tiled=True),
        lax.all_gather(decoder_weight.astype(jnp.bfloat16), "dp", axis=0, tiled=True),
    )
    attend_back, merge_back, up_back, down_back, encoder_back, decoder_back = regathered
    projected, log_sums, resid, hidden_pre = front(attend_back, merge_back, up_back)
    grad_hidden = jnp.dot(cotangent, down_back, preferred_element_type=jnp.float32)
    _, gelu_pull = jax.vjp(gelu_tanh, hidden_pre)
    grad_pre = gelu_pull(grad_hidden)[0].astype(jnp.bfloat16)
    up_part = jnp.einsum("tf,df->td", grad_pre, up_back, preferred_element_type=jnp.float32)
    grad_output = cotangent.astype(jnp.float32)
    up_total = lax.psum(up_part.astype(jnp.bfloat16), "tensor").astype(jnp.float32)
    grad_resid = grad_output + norm_back(resid, norm_params[2], norm_params[3], up_total)
    branch_grad = grad_resid.astype(jnp.bfloat16)
    grad_mixture = jnp.dot(branch_grad, merge_back, preferred_element_type=jnp.float32).astype(
        jnp.bfloat16
    )
    grad_mixture = grad_mixture.reshape(sequences, SEQ, local_heads, HD)

    def backward_sequence(items):
        seq_rows, grad_rows, seq_sums = items
        return attend_backward(
            seq_rows[:, 0],
            seq_rows[:, 1],
            seq_rows[:, 2],
            prefix_keys,
            prefix_values,
            grad_rows,
            seq_sums,
        )

    grad_seqs, grad_prefixes = lax.map(backward_sequence, (projected, grad_mixture, log_sums))
    grad_projected = grad_seqs.reshape(tok_rows, 3, local_width).astype(jnp.bfloat16)
    first_part = jnp.einsum(
        "tcm,dcm->td", grad_projected, attend_back, preferred_element_type=jnp.float32
    )
    first_total = lax.psum(first_part.astype(jnp.bfloat16), "tensor").astype(jnp.float32)
    input_full = grad_resid + norm_back(inputs, norm_params[0], norm_params[1], first_total)
    input_grad = lax.dynamic_slice_in_dim(input_full, row_start, share, 0)
    prefix_grad = jnp.sum(grad_prefixes, 0).reshape(PRE, 2, local_width)
    prefix_total = lax.psum(prefix_grad, "dp")
    prefix_low = prefix_total.astype(jnp.bfloat16)
    grad_decoder = jnp.einsum(
        "jp,jcm->pcm", hidden_low, prefix_low, preferred_element_type=jnp.float32
    )
    grad_decoder_bias = jnp.sum(prefix_low.astype(jnp.float32), 0)
    encoded_part = jnp.einsum(
        "jcm,pcm->jp", prefix_low, decoder_back, preferred_element_type=jnp.float32
    )
    square_part = jnp.sum(grad_decoder * grad_decoder) + jnp.sum(
        grad_decoder_bias * grad_decoder_bias
    )
    encoded_grad, square_decoder = lax.psum((encoded_part, square_part), "tensor")
    grad_encoded = (encoded_grad * (1.0 - hidden_prefix * hidden_prefix)).astype(jnp.bfloat16)
    grad_encoder = jnp.dot(selected_low.T, grad_encoded, preferred_element_type=jnp.float32)
    grad_encoder_bias = jnp.sum(grad_encoded.astype(jnp.float32), 0)
    grad_selected = jnp.dot(grad_encoded, encoder_back.T, preferred_element_type=jnp.float32)
    grad_table = jnp.dot(onehot.T, grad_selected, precision=highest_prec)
    squares = (
        square_decoder
        + jnp.sum(grad_table * grad_table)
        + jnp.sum(grad_encoder * grad_encoder)
        + jnp.sum(grad_encoder_bias * grad_encoder_bias)
    )
    grad_norm = jnp.sqrt(squares)
    factor = CLIP_LIMIT / (grad_norm + 1e-06)
    encoder_rows = encoder_weight.shape[0]
    decoder_rows = decoder_weight.shape[0]
    encoder_own = lax.dynamic_slice_in_dim(grad_encoder, dp_index * encoder_rows, encoder_rows, 0)
    decoder_own = lax.dynamic_slice_in_dim(grad_decoder, dp_index * decoder_rows, decoder_rows, 0)
    table_new = adam_update(prefix_table, grad_table, first_table, second_table, factor)
    encoder_new = adam_update(encoder_weight, encoder_own, first_encoder, second_encoder, factor)
    enc_bias_new = adam_update(
        encoder_bias, grad_encoder_bias, first_encoder_bias, second_encoder_bias, factor
    )
    decoder_new = adam_update(decoder_weight, decoder_own, first_decoder, second_decoder, factor)
    dec_bias_new = adam_update(
        decoder_bias, grad_decoder_bias, first_decoder_bias, second_decoder_bias, factor
    )
    return (
        output_rows.astype(jnp.bfloat16),
        input_grad.astype(jnp.bfloat16),
        grad_norm,
        table_new[0],
        table_new[1],
        table_new[2],
        encoder_new[0],
        encoder_new[1],
        encoder_new[2],
        enc_bias_new[0],
        enc_bias_new[1],
        enc_bias_new[2],
        decoder_new[0],
        decoder_new[1],
        decoder_new[2],
        dec_bias_new[0],
        dec_bias_new[1],
        dec_bias_new[2],
    )


def solution(mesh):
    in_specs = (
        P("dp", None),
        P("dp", None),
        P(),
        P("dp", None, "tensor"),
        P(None, "tensor"),
        P("dp", "tensor"),
        P(),
        P("dp", "tensor"),
        P("tensor"),
        P("dp", "tensor"),
        P(),
        P(),
        P("dp", None),
        P(),
        P("dp", None, "tensor"),
        P(None, "tensor"),
        P(),
        P(),
        P("dp", None),
        P("dp", None),
        P(),
        P(),
        P("dp", None, "tensor"),
        P("dp", None, "tensor"),
        P(None, "tensor"),
        P(None, "tensor"),
    )
    out_specs = (
        P(("dp", "tensor"), None),
        P(("dp", "tensor"), None),
        P(),
        P(),
        P(),
        P(),
        P("dp", None),
        P("dp", None),
        P("dp", None),
        P(),
        P(),
        P(),
        P("dp", None, "tensor"),
        P("dp", None, "tensor"),
        P("dp", None, "tensor"),
        P(None, "tensor"),
        P(None, "tensor"),
        P(None, "tensor"),
    )
    return jax.shard_map(
        on_device, mesh=mesh, in_specs=in_specs, out_specs=out_specs, check_vma=False
    )
```

profile of v0, /device:TPU:0, one launch (start us, length us, event | category | flops | bytes accessed | tf_op | source)
XLA Modules:
  0.0 530.9 jit_solution(5144852693320282007)
XLA Ops:
  15.7 34.4 %all_gather.25 = bf16[512,2,256]{2,0,1:T(8,128)(2,1)S(1)} all-gather(bf16[64,2,256]{2,0,1:T(8,128)(2,1)S(1)} %copy.110), channel_id=1, replica_groups=mesh['dp'=8,'tensor'=4] {'dp'}, dimensions={0}, use_global_device_ids=true | all-gather | bytes 589824 | tf_op jit(solution)/shard_map/all_gather | solution.py:198
  50.1 31.8 %all_gather.27 = bf16[1024,256]{1,0:T(8,128)(2,1)S(1)} all-gather(bf16[128,256]{1,0:T(8,128)(2,1)S(1)} %copy-done.46), channel_id=1, replica_groups=mesh['dp'=8,'tensor'=4] {'dp'}, dimensions={0}, use_global_device_ids=true | all-gather | bytes 589824 | tf_op jit(solution)/shard_map/all_gather | solution.py:194
  85.5 17.9 %all-gather.7.cloned.1.call-done = bf16[1024,3,256]{0,2,1:T(8,128)(2,1)} async-done(((bf16[128,3,256]{0,2,1:T(8,128)(2,1)}), bf16[1024,3,256]{0,2,1:T(8,128)(2,1)}) %all-gather.7.cloned.1.call-update) | async-done | bytes 1572880 | tf_op jit(solution)/shard_map/all_gather | solution.py:193
  103.4 3.4 add_convert_fusion.1
  116.1 2.5 fusion.21
  122.5 11.8 %all-reduce.10.cloned.1.call-start = ((), (), s32[]{:S(2)}) async-start(), calls=%async_computation.5 | async-start | bytes 4194304 | tf_op jit(solution)/shard_map/psum | solution.py:263
  134.9 36.1 %all-reduce.8.cloned.1.call-done = bf16[1024,1024]{1,0:T(8,128)(2,1)} async-done(((bf16[1024,1024]{1,0:T(8,128)(2,1)}), bf16[1024,1024]{1,0:T(8,128)(2,1)}) %all-reduce.8.cloned.1.call-update) | async-done | bytes 2097168 | tf_op jit(solution)/shard_map/psum | solution.py:233
  175.8 46.3 %all-gather.9.cloned.1.call-done = bf16[1024,1024]{1,0:T(8,128)(2,1)} async-done(((bf16[128,1024]{1,0:T(8,128)(2,1)}), bf16[1024,1024]{1,0:T(8,128)(2,1)}) %all-gather.9.cloned.1.call-update) | async-done | bytes 2097168 | tf_op jit(solution)/shard_map/all_gather | solution.py:195
  222.2 7.2 %fusion.26 = f32[1024,1024]{1,0:T(8,128)} fusion(bf16[1024,1024]{1,0:T(8,128)(2,1)} %all-gather.9.cloned.1.call-done, f32[1024,1024]{1,0:T(8,128)} %copy-done.1, f32[1024]{0:T(1024)S(1)} %bitcast.198, f32[1024]{0:T(1024)S(1)} %bitcast.189, f32[1024]{0:T(1024)S(1)} %fusion.124, f32[1024]{0:T(1024)S(1)} %broadcast_multiply_fusion), kind=kOutput, calls=%fused_computation.54 | convolution fusion | flops 2152726528 | bytes 10502144 | tf_op jit(solution)/shard_map/dot_general | solution.py:236
  229.4 42.4 %all-gather.11.cloned.1.call-done = bf16[1024,1024]{1,0:T(8,128)(2,1)} async-done(((bf16[128,1024]{1,0:T(8,128)(2,1)}), bf16[1024,1024]{1,0:T(8,128)(2,1)}) %all-gather.11.cloned.1.call-update) | async-done | bytes 2097168 | tf_op jit(solution)/shard_map/all_gather | solution.py:196
  271.8 10.8 %fusion.45 = bf16[1024,1024]{1,0:T(8,128)(2,1)} fusion(bf16[1024,1024]{1,0:T(8,128)(2,1)} %all-gather.9.cloned.1.call-done, f32[1024,1024]{1,0:T(8,128)} %fusion.26, f32[1024]{0:T(1024)S(1)} %copy-done.62, bf16[1024,1024]{1,0:T(8,128)(2,1)} %param.39, bf16[1024,1024]{1,0:T(8,128)(2,1)} %all-gather.11.cloned.1.call-done), kind=kOutput, calls=%fused_computation.73 | convolution fusion | flops 4322230272 | bytes 12587008 | tf_op jit(solution)/shard_map/tf,df->td/dot_general | solution.py:261
  282.7 7.0 %fusion.48 = bf16[1024,1024]{1,0:T(8,128)(2,1)} fusion(bf16[1024,1024]{1,0:T(8,128)(2,1)} %all-gather.11.cloned.1.call-done, f32[1024,1024]{1,0:T(8,128)} %fusion.26, f32[1024]{0:T(1024)S(1)} %copy-done.62), kind=kOutput, calls=%fused_computation.74 | convolution fusion | flops 2159017984 | bytes 8392704 | tf_op jit(solution)/shard_map/tf,df->td/dot_general | solution.py:241
  289.7 43.0 %all-reduce.10.cloned.1.call-done = bf16[1024,1024]{1,0:T(8,128)(2,1)} async-done(((bf16[1024,1024]{1,0:T(8,128)(2,1)}), bf16[1024,1024]{1,0:T(8,128)(2,1)}) %all-reduce.10.cloned.1.call-update) | async-done | bytes 2097168 | tf_op jit(solution)/shard_map/psum | solution.py:263
  332.7 3.8 multiply_reduce_fusion.2
  352.2 4.9 multiply_reduce_fusion
  361.9 37.1 %psum.56 = bf16[10,2,256]{2,0,1:T(8,128)(2,1)S(1)} all-reduce(f32[10,2,256]{2,0,1:T(8,128)S(1)} %pad_maximum_fusion.2), channel_id=1, replica_groups=mesh['dp'=8,'tensor'=4] {'dp'}, use_global_device_ids=true, to_apply=%region_24.25 | all-reduce | flops 5120 | bytes 30720 | tf_op jit(solution)/shard_map/psum | solution.py:292
  402.9 5.0 fusion.64
  409.9 6.8 %multiply_convert_fusion = bf16[4,512,1024]{2,1,0:T(8,128)(2,1)S(1)} fusion(f32[4,512,1024]{2,1,0:T(8,128)} %get-tuple-element.245, f32[4,512,1024]{2,1,0:T(8,128)} %copy-done, f32[4,512]{1,0:T(4,128)S(1)} %add.428, f32[4,512]{1,0:T(4,128)S(1)} %copy-done.27), kind=kLoop, calls=%fused_computation | loop fusion | flops 8388608 | bytes 20987904 | tf_op jit(solution)/shard_map/while/body/eval_jaxpr/convert_element_type | solution.py:120
  422.1 3.8 fusion.84
  427.4 4.9 bitcast_convert_fusion
  432.4 14.0 %all-reduce.2 = (f32[]{:T(128)}, f32[10,512]{1,0:T(8,128)}) all-reduce(f32[]{:T(128)S(6)} %add.438, f32[10,512]{1,0:T(8,128)} %convolution_bitcast_fusion), channel_id=1, replica_groups=mesh['dp'=8,'tensor'=4] {'tensor'}, use_global_device_ids=true, to_apply=%region_28.29 | all-reduce | flops 5121 | bytes 40968 | tf_op jit(solution)/shard_map/psum | solution.py:304
  465.9 49.0 %all-reduce.12.cloned.1.call-done = (bf16[1024,1024]{1,0:T(8,128)(2,1)}, bf16[1024,1024]{1,0:T(8,128)(2,1)}) async-done(((bf16[1024,1024]{1,0:T(8,128)(2,1)}, bf16[1024,1024]{1,0:T(8,128)(2,1)}), (bf16[1024,1024]{1,0:T(8,128)(2,1)}, bf16[1024,1024]{1,0:T(8,128)(2,1)})) %all-reduce.12.cloned.1.call-update) | async-done | bytes 4194320 | tf_op jit(solution)/shard_map/psum | solution.py:242
  514.8 2.7 fusion.14
  519.6 2.9 fusion.90
  (237 shorter events, 80.9 us)
Async XLA Ops:
  7.2 42.8 %copy-start.46 = (bf16[128,256]{1,0:T(8,128)(2,1)S(1)}, bf16[128,256]{1,0:T(8,128)(2,1)}, u32[]{:S(2)}) copy-start(bf16[128,256]{1,0:T(8,128)(2,1)} %param.43) | copy-start | bytes 196612
  7.2 75.8 %copy-start.58 = (f32[512]{0:T(512)S(1)}, f32[512]{0:T(512)}, u32[]{:S(2)}) copy-start(f32[512]{0:T(512)} %param.51) | copy-start | bytes 6148
  7.3 75.8 %all-gather.5.cloned.1.call-start = ((), (), s32[]{:S(2)}) async-start(), calls=%async_computation | async-start | bytes 1179648 | tf_op jit(solution)/shard_map/all_gather | solution.py:197
  9.1 76.1 %copy-start.57 = (f32[2,256]{1,0:T(2,128)S(1)}, f32[2,256]{1,0:T(2,128)}, u32[]{:S(2)}) copy-start(f32[2,256]{1,0:T(2,128)} %param.53) | copy-start | bytes 6148
  9.1 94.3 %all-gather.7.cloned.1.call-start = ((), (), s32[]{:S(2)}) async-start(), calls=%async_computation.1 | async-start | bytes 1769472 | tf_op jit(solution)/shard_map/all_gather | solution.py:193
  10.9 92.5 %copy-start.61 = (f32[3,256]{1,0:T(4,128)S(1)}, f32[3,256]{1,0:T(4,128)}, u32[]{:S(2)}) copy-start(f32[3,256]{1,0:T(4,128)} %param.42) | copy-start | bytes 9220
  10.9 160.1 %all-reduce.8.cloned.1.call-start = ((), (), s32[]{:S(2)}) async-start(), calls=%async_computation.2 | async-start | bytes 4194304 | tf_op jit(solution)/shard_map/psum | solution.py:233
  14.6 92.2 %copy-start.44 = (f32[1024]{0:T(1024)}, f32[1024]{0:T(1024)S(1)}, u32[]{:S(2)}) copy-start(f32[1024]{0:T(1024)S(1)} %broadcast_multiply_fusion.1) | copy-start | bytes 12292
  15.3 66.6 %copy-start.49 = (f32[1024]{0:T(1024)}, f32[1024]{0:T(1024)S(1)}, u32[]{:S(2)}) copy-start(f32[1024]{0:T(1024)S(1)} %fusion.10) | copy-start | bytes 12292
  15.4 91.5 %copy-start.53 = (f32[1024]{0:T(1024)}, f32[1024]{0:T(1024)S(1)}, u32[]{:S(2)}) copy-start(f32[1024]{0:T(1024)S(1)} %fusion.123) | copy-start | bytes 12292
  15.4 91.4 %copy-start.47 = (f32[1,1024]{1,0:T(1,128)}, f32[1,1024]{1,0:T(1,128)S(1)}, u32[]{:S(2)}) copy-start(f32[1,1024]{1,0:T(1,128)S(1)} %get-tuple-element.230) | copy-start | bytes 12292
  15.6 91.2 %copy-start.30 = (bf16[10,1024]{1,0:T(8,128)(2,1)}, bf16[10,1024]{1,0:T(8,128)(2,1)S(1)}, u32[]{:S(2)}) copy-start(bf16[10,1024]{1,0:T(8,128)(2,1)S(1)} %convolution_convert_fusion.1) | copy-start | bytes 61444
  121.3 100.9 %all-gather.9.cloned.1.call-start = ((), (), s32[]{:S(2)}) async-start(), calls=%async_computation.3 | async-start | bytes 2359296 | tf_op jit(solution)/shard_map/all_gather | solution.py:195
  121.9 149.9 %all-gather.11.cloned.1.call-start = ((), (), s32[]{:S(2)}) async-start(), calls=%async_computation.4 | async-start | bytes 2359296 | tf_op jit(solution)/shard_map/all_gather | solution.py:196
  122.5 210.2 %all-reduce.10.cloned.1.call-start = ((), (), s32[]{:S(2)}) async-start(), calls=%async_computation.5 | async-start | bytes 4194304 | tf_op jit(solution)/shard_map/psum | solution.py:263
  222.2 49.6 %copy-start.62 = (f32[1024]{0:T(1024)S(1)}, f32[1024]{0:T(1024)}, u32[]{:S(2)}) copy-start(f32[1024]{0:T(1024)} %param.46) | copy-start | bytes 12292
  282.6 232.2 %all-reduce.12.cloned.1.call-start = ((), (), s32[]{:S(2)}) async-start(), calls=%async_computation.6 | async-start | bytes 8388608 | tf_op jit(solution)/shard_map/psum | solution.py:242
  352.2 47.8 %copy-start.40 = (bf16[10,1,4,64]{3,2,0,1:T(4,128)(2,1)S(1)}, bf16[10,1,4,64]{3,2,0,1:T(4,128)(2,1)}, u32[]{:S(2)}) copy-start(bf16[10,1,4,64]{3,2,0,1:T(4,128)(2,1)} %copy-done.39) | copy-start | bytes 15364
  352.2 48.8 %copy-start.23 = (f32[10,512]{1,0:T(8,128)S(1)}, f32[10,512]{1,0:T(8,128)}, u32[]{:S(2)}) copy-start(f32[10,512]{1,0:T(8,128)} %copy-done.22) | copy-start | bytes 61444
  357.1 45.8 %copy-start.27 = (f32[4,512]{1,0:T(4,128)S(1)}, f32[4,512]{1,0:T(4,128)}, u32[]{:S(2)}) copy-start(f32[4,512]{1,0:T(4,128)} %get-tuple-element.220) | copy-start | bytes 24580
  453.5 64.1 %copy-start.50 = (f32[1024]{0:T(1024)S(1)}, f32[1024]{0:T(1024)}, u32[]{:S(2)}) copy-start(f32[1024]{0:T(1024)} %copy-done.49) | copy-start | bytes 12292
  453.5 64.1 %copy-start.45 = (f32[1024]{0:T(1024)S(1)}, f32[1024]{0:T(1024)}, u32[]{:S(2)}) copy-start(f32[1024]{0:T(1024)} %copy-done.44) | copy-start | bytes 12292
  453.5 64.1 %copy-start.48 = (f32[1,1024]{1,0:T(1,128)S(1)}, f32[1,1024]{1,0:T(1,128)}, u32[]{:S(2)}) copy-start(f32[1,1024]{1,0:T(1,128)} %copy-done.47) | copy-start | bytes 12292
  453.5 64.1 %copy-start.54 = (f32[1024]{0:T(1024)S(1)}, f32[1024]{0:T(1024)}, u32[]{:S(2)}) copy-start(f32[1024]{0:T(1024)} %copy-done.53) | copy-start | bytes 12292
  (48 other events, 381.8 us)
Sparse Core Ops, SparseCore 0:
  10.8 46.0 all-gather.4
  59.5 43.8 all-gather.6
  121.4 49.5 all-reduce.7
  173.0 49.1 all-gather.8
  224.2 47.6 all-gather.10
  282.7 49.9 all-reduce.9
  432.5 82.2 all-reduce.11
where the time goes:
time: 540 us; the launch traced here: 531 us
  waiting for transfers between devices  236 us (44%)
  blocking collectives  117 us (22%)
  matrix products  78.6 us (15%)
  other arithmetic  49.2 us (9%)
  between operations  20.5 us (4%)
  local copies, waits for them, and re-layouts  17.3 us (3%)
  starting transfers between devices  12.1 us (2%)
    psum x1, waiting for transfers between devices, on_device(): lax.psum(branch_part.astype(jnp.bfloat16), 'tensor').astype(jnp.float32)  49 us
    all_gather x1, waiting for transfers between devices, on_device(): lax.all_gather(up_weight, 'dp', axis=0, tiled=True)  46.3 us
    psum x1, waiting for transfers between devices, on_device(): lax.psum(up_part.astype(jnp.bfloat16), 'tensor').astype(jnp.float32)  43 us
    all_gather x1, waiting for transfers between devices, on_device(): lax.all_gather(down_weight, 'dp', axis=0, tiled=True)  42.4 us
    psum x1, blocking collectives, on_device(): prefix_total = lax.psum(prefix_grad, 'dp')  37.1 us
    psum x1, waiting for transfers between devices, front(): lax.psum(merged_part.astype(jnp.bfloat16), 'tensor').astype(jnp.float32)  36.1 us
    all_gather x1, blocking collectives, on_device(): lax.all_gather(decoder_weight.astype(jnp.bfloat16), 'dp', axis=0, tiled=T...  34.4 us
    all_gather x1, blocking collectives, on_device(): lax.all_gather(merge_weight, 'dp', axis=0, tiled=True)  31.8 us
  transfers between devices with their start and end apart: 7, of which 6 were waited for; matrix products, arithmetic and copies ran while one was open for 8% of the time, Pallas kernels for 0%

commit v1 on v0

--- a/solution.py
+++ b/solution.py
@@ -16,6 +16,32 @@
 ADAM_EPS = 1e-08
 MASKED = -1e30
 GELU_COEF = 0.7978845608028654
+
+
+def pass_trees(body, axis_no):
+    w1 = list(body.shape[1:])
+    w1[axis_no] *= body.shape[0]
+    return jnp.moveaxis(body, 0, axis_no).reshape(w1)
+
+
+def unite_group_on(original, device_axis, array_axis):
+    chips = lax.axis_size(device_axis)
+    copies = tuple(((ii, (ii + 1) % chips) for ii in range(chips)))
+    parts_seen = tuple(((j0, tick) for tick, j0 in copies))
+    z, newest = ([], [])
+    d = 0
+    while d < chips - 1:
+        if d % 2 == 0:
+            z.append(lax.ppermute(z[-1] if z else original, device_axis, perm=copies))
+        else:
+            newest.append(
+                lax.ppermute(newest[-1] if newest else original, device_axis, perm=parts_seen)
+            )
+        d += 1
+    arr_next = jnp.stack([*z[::-1], original, *newest], 0)
+    seen_now = lax.axis_index(device_axis) - len(z)
+    arr_next = arr_next[(jnp.arange(chips) - seen_now) % chips]
+    return pass_trees(arr_next, array_axis)
 
 
 def layer_norm(rows, gain, shift):
@@ -195,7 +221,7 @@
         lax.all_gather(up_weight, "dp", axis=0, tiled=True),
         lax.all_gather(down_weight, "dp", axis=0, tiled=True),
         lax.all_gather(encoder_weight.astype(jnp.bfloat16), "dp", axis=0, tiled=True),
-        lax.all_gather(decoder_weight.astype(jnp.bfloat16), "dp", axis=0, tiled=True),
+        unite_group_on(decoder_weight.astype(jnp.bfloat16), "dp", 0),
     )
     attend_full, merge_full, up_full, down_full, encoder_full, decoder_full = gathered
     onehot = (prefix_ids[:, None] == jnp.arange(PRE, dtype=jnp.int32)[None, :]).astype(jnp.float32)

time: 540 us -> 544 us (level)
  waiting for transfers between devices: 236 us -> 214 us
  starting transfers between devices: 12.1 us -> 29.9 us
    psum x1, waiting for transfers between devices: 43 us -> 9.66 us  [on_device(): lax.psum(up_part.astype(jnp.bfloat16), 'tensor').astype(jnp.float32)]
    ppermute x0 -> x7, starting transfers between devices: none -> 17.5 us  [the longest x3 16 us: unite_group_on(): lax.ppermute(newest[-1] if newest else original, device_axis, perm=parts_...]
    all_gather x1, starting transfers between devices: 0.04 us -> 12.1 us  [on_device(): lax.all_gather(up_weight, 'dp', axis=0, tiled=True)]
    psum x1, starting transfers between devices: 11.8 us -> 0.04 us  [on_device(): lax.psum(up_part.astype(jnp.bfloat16), 'tensor').astype(jnp.float32)]
    ppermute x0 -> x7, waiting for transfers between devices: none -> 9.15 us  [the longest x4 8.78 us: unite_group_on(): z.append(lax.ppermute(z[-1] if z else original, device_axis, perm=copies))]
    unnamed x135 -> x130, local copies, waits for them, and re-layouts: 13.4 us -> 12.5 us
  transfers between devices with their start and end apart: 7 -> 14, of which waited for: 6 -> 10; matrix products, arithmetic and copies ran while one was open for 8% -> 9% of each run, Pallas kernels for 0% -> 0%
where the time goes in v1:
time: 544 us; the launch traced here: 534 us
  waiting for transfers between devices  214 us (39%)
  blocking collectives  117 us (22%)
  matrix products  80.8 us (15%)
  other arithmetic  50.6 us (9%)
  starting transfers between devices  29.9 us (5%)
  local copies, waits for them, and re-layouts  21.5 us (4%)
  between operations  20.6 us (4%)
    psum x1, waiting for transfers between devices, on_device(): lax.psum(branch_part.astype(jnp.bfloat16), 'tensor').astype(jnp.float32)  48.2 us
    all_gather x1, waiting for transfers between devices, on_device(): lax.all_gather(up_weight, 'dp', axis=0, tiled=True)  46.3 us
    all_gather x1, waiting for transfers between devices, on_device(): lax.all_gather(down_weight, 'dp', axis=0, tiled=True)  42.4 us
    psum x1, blocking collectives, on_device(): prefix_total = lax.psum(prefix_grad, 'dp')  37.1 us
    psum x1, waiting for transfers between devices, front(): lax.psum(merged_part.astype(jnp.bfloat16), 'tensor').astype(jnp.float32)  35.5 us
    all_gather x1, blocking collectives, on_device(): lax.all_gather(decoder_weight.astype(jnp.bfloat16), 'dp', axis=0, tiled=T...  33.3 us
    all_gather x1, blocking collectives, on_device(): lax.all_gather(merge_weight, 'dp', axis=0, tiled=True)  32.6 us
    all_gather x1, waiting for transfers between devices, on_device(): lax.all_gather(attention_weight, 'dp', axis=0, tiled=True)  22 us
  transfers between devices with their start and end apart: 14, of which 10 were waited for; matrix products, arithmetic and copies ran while one was open for 9% of the time, Pallas kernels for 0%

profile of v1, /device:TPU:0, one launch (start us, length us, event | category | flops | bytes accessed | tf_op | source)
XLA Modules:
  0.0 534.4 jit_solution(17664728354706680140)
XLA Ops:
  10.1 6.1 %collective-permute-start.4 = (bf16[64,2,256]{2,0,1:T(8,128)(2,1)S(1)}, bf16[64,2,256]{2,0,1:T(8,128)(2,1)S(1)}, u32[]{:S(2)}, u32[]{:S(2)}) collective-permute-start(bf16[64,2,256]{2,0,1:T(8,128)(2,1)S(1)} %copy.111), channel_id=1, source_target_pairs={{4,0},{8,4},{12,8},{16,12},{20,16},{24,20},{28,24},{0,28},{5,1},{9... | collective-permute-start | bytes 196616 | tf_op jit(solution)/shard_map/ppermute | solution.py:38
  22.5 32.6 %all_gather.25 = bf16[1024,256]{1,0:T(8,128)(2,1)S(1)} all-gather(bf16[128,256]{1,0:T(8,128)(2,1)S(1)} %copy-done.39), channel_id=1, replica_groups=mesh['dp'=8,'tensor'=4] {'dp'}, dimensions={0}, use_global_device_ids=true | all-gather | bytes 589824 | tf_op jit(solution)/shard_map/all_gather | solution.py:220
  57.6 5.0 collective-permute-done.1
  62.7 4.8 collective-permute-start.5
  70.1 5.2 collective-permute-start.6
  82.9 22.0 %all-gather.7.cloned.1.call-done = bf16[1024,3,256]{0,2,1:T(8,128)(2,1)} async-done(((bf16[128,3,256]{0,2,1:T(8,128)(2,1)}), bf16[1024,3,256]{0,2,1:T(8,128)(2,1)}) %all-gather.7.cloned.1.call-update) | async-done | bytes 1572880 | tf_op jit(solution)/shard_map/all_gather | solution.py:219
  122.8 12.1 %all-gather.9.cloned.1.call-start = ((), (), s32[]{:S(2)}) async-start(), calls=%async_computation.3 | async-start | bytes 2359296 | tf_op jit(solution)/shard_map/all_gather | solution.py:221
  137.0 35.5 %all-reduce.8.cloned.1.call-done = bf16[1024,1024]{1,0:T(8,128)(2,1)} async-done(((bf16[1024,1024]{1,0:T(8,128)(2,1)}), bf16[1024,1024]{1,0:T(8,128)(2,1)}) %all-reduce.8.cloned.1.call-update) | async-done | bytes 2097168 | tf_op jit(solution)/shard_map/psum | solution.py:259
  177.4 46.3 %all-gather.9.cloned.1.call-done = bf16[1024,1024]{1,0:T(8,128)(2,1)} async-done(((bf16[128,1024]{1,0:T(8,128)(2,1)}), bf16[1024,1024]{1,0:T(8,128)(2,1)}) %all-gather.9.cloned.1.call-update) | async-done | bytes 2097168 | tf_op jit(solution)/shard_map/all_gather | solution.py:221
  223.7 7.2 %fusion.26 = f32[1024,1024]{1,0:T(8,128)} fusion(bf16[1024,1024]{1,0:T(8,128)(2,1)} %all-gather.9.cloned.1.call-done, f32[1024,1024]{1,0:T(8,128)} %copy-done.1, f32[1024]{0:T(1024)S(1)} %bitcast.218, f32[1024]{0:T(1024)S(1)} %bitcast.209, f32[1024]{0:T(1024)S(1)} %fusion.124, f32[1024]{0:T(1024)S(1)} %broadcast_multiply_fusion), kind=kOutput, calls=%fused_computation.55 | convolution fusion | flops 2152726528 | bytes 10502144 | tf_op jit(solution)/shard_map/dot_general | solution.py:262
  230.9 42.4 %all-gather.11.cloned.1.call-done = bf16[1024,1024]{1,0:T(8,128)(2,1)} async-done(((bf16[128,1024]{1,0:T(8,128)(2,1)}), bf16[1024,1024]{1,0:T(8,128)(2,1)}) %all-gather.11.cloned.1.call-update) | async-done | bytes 2097168 | tf_op jit(solution)/shard_map/all_gather | solution.py:222
  273.3 10.8 %fusion.45 = bf16[1024,1024]{1,0:T(8,128)(2,1)} fusion(bf16[1024,1024]{1,0:T(8,128)(2,1)} %all-gather.9.cloned.1.call-done, f32[1024,1024]{1,0:T(8,128)} %fusion.26, f32[1024]{0:T(1024)S(1)} %copy-done.56, bf16[1024,1024]{1,0:T(8,128)(2,1)} %param.39, bf16[1024,1024]{1,0:T(8,128)(2,1)} %all-gather.11.cloned.1.call-done), kind=kOutput, calls=%fused_computation.74 | convolution fusion | flops 4322230272 | bytes 12587008 | tf_op jit(solution)/shard_map/tf,df->td/dot_general | solution.py:287
  284.2 33.3 %all_gather.28 = bf16[512,2,256]{2,0,1:T(8,128)(2,1)} all-gather(bf16[64,2,256]{2,0,1:T(8,128)(2,1)S(1)} %copy-done.31), channel_id=1, replica_groups=mesh['dp'=8,'tensor'=4] {'dp'}, dimensions={0}, use_global_device_ids=true | all-gather | bytes 589824 | tf_op jit(solution)/shard_map/all_gather | solution.py:280
  317.4 7.1 %fusion.48 = bf16[1024,1024]{1,0:T(8,128)(2,1)} fusion(bf16[1024,1024]{1,0:T(8,128)(2,1)} %all-gather.11.cloned.1.call-done, f32[1024,1024]{1,0:T(8,128)} %fusion.26, f32[1024]{0:T(1024)S(1)} %copy-done.56), kind=kOutput, calls=%fused_computation.75 | convolution fusion | flops 2159017984 | bytes 8392704 | tf_op jit(solution)/shard_map/tf,df->td/dot_general | solution.py:267
  324.5 9.7 %all-reduce.10.cloned.1.call-done = bf16[1024,1024]{1,0:T(8,128)(2,1)} async-done(((bf16[1024,1024]{1,0:T(8,128)(2,1)}), bf16[1024,1024]{1,0:T(8,128)(2,1)}) %all-reduce.10.cloned.1.call-update) | async-done | bytes 2097168 | tf_op jit(solution)/shard_map/psum | solution.py:289
  334.2 3.8 multiply_reduce_fusion.2
  352.8 4.9 multiply_reduce_fusion
  366.3 37.1 %psum.56 = bf16[10,2,256]{2,0,1:T(8,128)(2,1)S(1)} all-reduce(f32[10,2,256]{2,0,1:T(8,128)S(1)} %pad_maximum_fusion.2), channel_id=1, replica_groups=mesh['dp'=8,'tensor'=4] {'dp'}, use_global_device_ids=true, to_apply=%region_24.25 | all-reduce | flops 5120 | bytes 30720 | tf_op jit(solution)/shard_map/psum | solution.py:318
  406.7 4.8 fusion.64
  414.0 6.8 %multiply_convert_fusion = bf16[4,512,1024]{2,1,0:T(8,128)(2,1)S(1)} fusion(f32[4,512,1024]{2,1,0:T(8,128)} %get-tuple-element.245, f32[4,512,1024]{2,1,0:T(8,128)} %copy-done, f32[4,512]{1,0:T(4,128)S(1)} %add.454, f32[4,512]{1,0:T(4,128)S(1)} %copy-done.22), kind=kLoop, calls=%fused_computation.1 | loop fusion | flops 8388608 | bytes 20987904 | tf_op jit(solution)/shard_map/while/body/eval_jaxpr/convert_element_type | solution.py:146
  425.7 3.8 fusion.84
  431.0 4.9 bitcast_convert_fusion
  435.9 14.0 %all-reduce.2 = (f32[]{:T(128)}, f32[10,512]{1,0:T(8,128)}) all-reduce(f32[]{:T(128)S(6)} %add.464, f32[10,512]{1,0:T(8,128)} %convolution_bitcast_fusion), channel_id=1, replica_groups=mesh['dp'=8,'tensor'=4] {'tensor'}, use_global_device_ids=true, to_apply=%region_28.29 | all-reduce | flops 5121 | bytes 40968 | tf_op jit(solution)/shard_map/psum | solution.py:330
  470.1 48.2 %all-reduce.12.cloned.1.call-done = (bf16[1024,1024]{1,0:T(8,128)(2,1)}, bf16[1024,1024]{1,0:T(8,128)(2,1)}) async-done(((bf16[1024,1024]{1,0:T(8,128)(2,1)}, bf16[1024,1024]{1,0:T(8,128)(2,1)}), (bf16[1024,1024]{1,0:T(8,128)(2,1)}, bf16[1024,1024]{1,0:T(8,128)(2,1)})) %all-reduce.12.cloned.1.call-update) | async-done | bytes 4194320 | tf_op jit(solution)/shard_map/psum | solution.py:268
  (251 shorter events, 105.4 us)
Async XLA Ops:
  7.2 70.5 %copy-start.17 = (f32[64,2,256]{2,1,0:T(2,128)S(1)}, f32[64,2,256]{2,1,0:T(2,128)}, u32[]{:S(2)}) copy-start(f32[64,2,256]{2,1,0:T(2,128)} %param.52) | copy-start | bytes 393220
  7.3 73.8 %all-gather.5.cloned.1.call-start = ((), (), s32[]{:S(2)}) async-start(), calls=%async_computation | async-start | bytes 1179648 | tf_op jit(solution)/shard_map/all_gather | solution.py:223
  9.1 95.8 %all-gather.7.cloned.1.call-start = ((), (), s32[]{:S(2)}) async-start(), calls=%async_computation.1 | async-start | bytes 1769472 | tf_op jit(solution)/shard_map/all_gather | solution.py:219
  10.1 69.9 %copy-start.30 = (bf16[64,2,256]{2,0,1:T(8,128)(2,1)}, bf16[64,2,256]{2,0,1:T(8,128)(2,1)S(1)}, u32[]{:S(2)}) copy-start(bf16[64,2,256]{2,0,1:T(8,128)(2,1)S(1)} %copy.111) | copy-start | bytes 196612
  10.1 52.6 %collective-permute-start.4 = (bf16[64,2,256]{2,0,1:T(8,128)(2,1)S(1)}, bf16[64,2,256]{2,0,1:T(8,128)(2,1)S(1)}, u32[]{:S(2)}, u32[]{:S(2)}) collective-permute-start(bf16[64,2,256]{2,0,1:T(8,128)(2,1)S(1)} %copy.111), channel_id=1, source_target_pairs={{4,0},{8,4},{12,8},{16,12},{20,16},{24,20},{28,24},{0,28},{5,1},{9... | collective-permute-start | bytes 196616 | tf_op jit(solution)/shard_map/ppermute | solution.py:38
  16.2 39.2 %collective-permute-start = (bf16[64,2,256]{2,0,1:T(8,128)(2,1)S(1)}, bf16[64,2,256]{2,0,1:T(8,128)(2,1)S(1)}, u32[]{:S(2)}, u32[]{:S(2)}) collective-permute-start(bf16[64,2,256]{2,0,1:T(8,128)(2,1)S(1)} %copy.111), channel_id=1, source_target_pairs={{0,4},{4,8},{8,12},{12,16},{16,20},{20,24},{24,28},{28,0},{1,5},{5... | collective-permute-start | bytes 196616 | tf_op jit(solution)/shard_map/ppermute | solution.py:35
  17.9 154.6 %all-reduce.8.cloned.1.call-start = ((), (), s32[]{:S(2)}) async-start(), calls=%async_computation.2 | async-start | bytes 4194304 | tf_op jit(solution)/shard_map/psum | solution.py:259
  18.0 63.0 %copy-start.52 = (f32[512]{0:T(512)S(1)}, f32[512]{0:T(512)}, u32[]{:S(2)}) copy-start(f32[512]{0:T(512)} %param.51) | copy-start | bytes 6148
  20.0 84.9 %copy-start.37 = (f32[1024]{0:T(1024)}, f32[1024]{0:T(1024)S(1)}, u32[]{:S(2)}) copy-start(f32[1024]{0:T(1024)S(1)} %broadcast_multiply_fusion.1) | copy-start | bytes 12292
  20.0 84.9 %copy-start.55 = (f32[3,256]{1,0:T(4,128)S(1)}, f32[3,256]{1,0:T(4,128)}, u32[]{:S(2)}) copy-start(f32[3,256]{1,0:T(4,128)} %param.42) | copy-start | bytes 9220
  21.3 87.0 %copy-start.42 = (f32[1,1024]{1,0:T(1,128)}, f32[1,1024]{1,0:T(1,128)S(1)}, u32[]{:S(2)}) copy-start(f32[1,1024]{1,0:T(1,128)S(1)} %get-tuple-element.230) | copy-start | bytes 12292
  55.4 7.3 %collective-permute-start.1 = (bf16[64,2,256]{2,0,1:T(8,128)(2,1)S(1)}, bf16[64,2,256]{2,0,1:T(8,128)(2,1)S(1)}, u32[]{:S(2)}, u32[]{:S(2)}) collective-permute-start(bf16[64,2,256]{2,0,1:T(8,128)(2,1)S(1)} %collective-permute-done), channel_id=1, source_target_pairs={{0,4},{4,8},{8,12},{12,16},{16,20},{20,24},{24,28},{28,0},{1,5},{5... | collective-permute-start | bytes 196616 | tf_op jit(solution)/shard_map/ppermute | solution.py:35
  62.6 7.1 %collective-permute-start.2 = (bf16[64,2,256]{2,0,1:T(8,128)(2,1)S(1)}, bf16[64,2,256]{2,0,1:T(8,128)(2,1)S(1)}, u32[]{:S(2)}, u32[]{:S(2)}) collective-permute-start(bf16[64,2,256]{2,0,1:T(8,128)(2,1)S(1)} %collective-permute-done.1), channel_id=1, source_target_pairs={{0,4},{4,8},{8,12},{12,16},{16,20},{20,24},{24,28},{28,0},{1,5},{5... | collective-permute-start | bytes 196616 | tf_op jit(solution)/shard_map/ppermute | solution.py:35
  62.7 7.4 %collective-permute-start.5 = (bf16[64,2,256]{2,0,1:T(8,128)(2,1)S(1)}, bf16[64,2,256]{2,0,1:T(8,128)(2,1)S(1)}, u32[]{:S(2)}, u32[]{:S(2)}) collective-permute-start(bf16[64,2,256]{2,0,1:T(8,128)(2,1)S(1)} %collective-permute-done.4), channel_id=1, source_target_pairs={{4,0},{8,4},{12,8},{16,12},{20,16},{24,20},{28,24},{0,28},{5,1},{9... | collective-permute-start | bytes 196616 | tf_op jit(solution)/shard_map/ppermute | solution.py:38
  69.7 7.1 %collective-permute-start.3 = (bf16[64,2,256]{2,0,1:T(8,128)(2,1)S(1)}, bf16[64,2,256]{2,0,1:T(8,128)(2,1)S(1)}, u32[]{:S(2)}, u32[]{:S(2)}) collective-permute-start(bf16[64,2,256]{2,0,1:T(8,128)(2,1)S(1)} %collective-permute-done.2), channel_id=1, source_target_pairs={{0,4},{4,8},{8,12},{12,16},{16,20},{20,24},{24,28},{28,0},{1,5},{5... | collective-permute-start | bytes 196616 | tf_op jit(solution)/shard_map/ppermute | solution.py:35
  70.1 8.4 %collective-permute-start.6 = (bf16[64,2,256]{2,0,1:T(8,128)(2,1)S(1)}, bf16[64,2,256]{2,0,1:T(8,128)(2,1)S(1)}, u32[]{:S(2)}, u32[]{:S(2)}) collective-permute-start(bf16[64,2,256]{2,0,1:T(8,128)(2,1)S(1)} %collective-permute-done.5), channel_id=1, source_target_pairs={{4,0},{8,4},{12,8},{16,12},{20,16},{24,20},{28,24},{0,28},{5,1},{9... | collective-permute-start | bytes 196616 | tf_op jit(solution)/shard_map/ppermute | solution.py:38
  122.8 100.9 %all-gather.9.cloned.1.call-start = ((), (), s32[]{:S(2)}) async-start(), calls=%async_computation.3 | async-start | bytes 2359296 | tf_op jit(solution)/shard_map/all_gather | solution.py:221
  135.0 138.4 %all-gather.11.cloned.1.call-start = ((), (), s32[]{:S(2)}) async-start(), calls=%async_computation.4 | async-start | bytes 2359296 | tf_op jit(solution)/shard_map/all_gather | solution.py:222
  135.5 198.6 %all-reduce.10.cloned.1.call-start = ((), (), s32[]{:S(2)}) async-start(), calls=%async_computation.5 | async-start | bytes 4194304 | tf_op jit(solution)/shard_map/psum | solution.py:289
  284.1 234.2 %all-reduce.12.cloned.1.call-start = ((), (), s32[]{:S(2)}) async-start(), calls=%async_computation.6 | async-start | bytes 8388608 | tf_op jit(solution)/shard_map/psum | solution.py:268
  457.8 63.3 %copy-start.45 = (f32[1024]{0:T(1024)S(1)}, f32[1024]{0:T(1024)}, u32[]{:S(2)}) copy-start(f32[1024]{0:T(1024)} %copy-done.44) | copy-start | bytes 12292
  457.8 63.3 %copy-start.38 = (f32[1024]{0:T(1024)S(1)}, f32[1024]{0:T(1024)}, u32[]{:S(2)}) copy-start(f32[1024]{0:T(1024)} %copy-done.37) | copy-start | bytes 12292
  457.8 63.3 %copy-start.43 = (f32[1,1024]{1,0:T(1,128)S(1)}, f32[1,1024]{1,0:T(1,128)}, u32[]{:S(2)}) copy-start(f32[1,1024]{1,0:T(1,128)} %copy-done.42) | copy-start | bytes 12292
  457.8 63.3 %copy-start.48 = (f32[1024]{0:T(1024)S(1)}, f32[1024]{0:T(1024)}, u32[]{:S(2)}) copy-start(f32[1024]{0:T(1024)} %copy-done.47) | copy-start | bytes 12292
  (49 other events, 803.0 us)
Sparse Core Ops, SparseCore 0:
  10.8 45.4 all-gather.4
  58.9 45.9 all-gather.6
  122.9 49.5 all-reduce.7
  174.5 49.1 all-gather.8
  225.7 47.6 all-gather.10
  284.2 49.9 all-reduce.9
  436.0 82.2 all-reduce.11
